TPU v7x, 512 devices: a 4x2x32 block of a 4x8x32 slice. The times are simulated.
512 devices in a mesh: groups: 2 (over y), pix: 32 (over z), sub: 4 (over x), rep: 2 (over core).
Axes of the slice: x: 4, y: 2, z: 32, core: 2. Of those that a mesh axis runs over, the one named last changes fastest.
The devices are a block of a 4x8x32 slice.
Arguments:
- gaia_pos: float32 [2, 65536], P(None, ('groups', 'pix', 'sub', 'rep')), parts along dimension 1, may hold values from 0 to 1
- gaia_shape: float32 [2, 65536], P(None, ('groups', 'pix', 'sub', 'rep')), parts along dimension 1, may hold values from 0.15 to 0.6
- gaia_corr: float32 [65536], P(('groups', 'pix', 'sub', 'rep')), parts along dimension 0, may hold values from -0.8 to 0.8
- gaia_dest: int32 [65536, 1], P(('groups', 'pix', 'sub', 'rep')), parts along dimension 0, may hold values from 0 to 127; in each aligned block of 128 rows (0 to 127, 128 to 255, ...) at most 2 rows name the same one
- gaia_cell: int32 [65536], P(('groups', 'pix', 'sub', 'rep')), parts along dimension 0, may hold values from 0 to 127
- wise_pos: float32 [2, 65536], P(None, ('groups', 'pix', 'sub', 'rep')), parts along dimension 1, may hold values from 0 to 1
- wise_shape: float32 [2, 65536], P(None, ('groups', 'pix', 'sub', 'rep')), parts along dimension 1, may hold values from 0.15 to 0.6
- wise_corr: float32 [65536], P(('groups', 'pix', 'sub', 'rep')), parts along dimension 0, may hold values from -0.8 to 0.8
- wise_dest: int32 [65536, 1], P(('groups', 'pix', 'sub', 'rep')), parts along dimension 0, may hold values from 0 to 127; in each aligned block of 128 rows (0 to 127, 128 to 255, ...) at most 2 rows name the same one
- wise_cell: int32 [65536], P(('groups', 'pix', 'sub', 'rep')), parts along dimension 0, may hold values from 0 to 127
Outputs:
- gaia_like: float32 [65536], P(('groups', 'pix', 'sub', 'rep')), parts along dimension 0
- gaia_offset: float32 [2, 65536], P(None, ('groups', 'pix', 'sub', 'rep')), parts along dimension 1
- wise_like: float32 [65536], P(('groups', 'pix', 'sub', 'rep')), parts along dimension 0
There are 2 independent parts, one for each index of `groups`. A program takes and returns all parts, laid end to end along the dimension named above; each array names one. Nothing has to cross between parts.
Inputs may be any that keep to these rules, and one draw needn't show every extreme that they name: `gaia_dest`: among the 128 sources of one device no target appears more than 2 times, and some target appears exactly 2 times; the owner of a source is dest // 4. `wise_dest`: among the 128 sources of one device no target appears more than 2 times, and some target appears exactly 2 times; the owner of a source is dest // 4. `gaia_cell`: pixel row inside the band is cell // 64, column cell % 64. `wise_cell`: pixel row inside the band is cell // 64, column cell % 64.
All inputs are finite; a program needn't handle non-finite values.
Results may differ from a plain program's by a relative error of at most 0.0003.
Values sent between devices are 32-bit elements; how exact they have to be, the bound alone decides.
No kernel may reach another device: no remote copies, remote signals or barrier semaphores. Data moves between devices by JAX's collectives and lax.ppermute only.
A program may use at most 64 MiB of HBM per device.

v0:
```python
import jax
import jax.numpy as jnp
from jax import lax
from jax.sharding import PartitionSpec as P

SRC_DEV = 128
BAND = 2
NCOL = 64


empty_gaia = -1000.0
empty_wise = -3000.0
row_offset = 4.0
inv_two_pi = 0.15915494309189535


def side_by_side(arrays, axis, split_dim, concat_dim, along):
    ends, at = ([], 0)
    for a in arrays[:-1]:
        at += a.shape[along]
        ends.append(at)
    both = jnp.concatenate(arrays, axis=along)
    return tuple(
        jnp.split(
            lax.all_to_all(both, axis, split_axis=split_dim, concat_axis=concat_dim, tiled=True),
            ends,
            axis=along,
        )
    )


def with_halo(x, sides, width):
    for axis, dim in sides:
        size, length = (lax.axis_size(axis), x.shape[dim])
        up = [(i, (i + 1) % size) for i in range(size - 1)]
        down = [(j, i) for i, j in up]
        last = lax.slice_in_dim(x, length - width, length, axis=dim)
        leading = lax.slice_in_dim(x, 0, width, axis=dim)
        before = lax.ppermute(last, axis, up)
        after = lax.ppermute(leading, axis, down)
        x = jnp.concatenate([before, x, after], axis=dim)
    return x


def from_everyone(x, axis):
    size = lax.axis_size(axis)
    return lax.all_to_all(jnp.broadcast_to(x[None], (size, *x.shape)), axis, 0, 0, tiled=True)


def joined_along(parts, dim):
    parts = jnp.moveaxis(parts, 0, dim)
    shape = parts.shape
    return parts.reshape(*shape[:dim], shape[dim] * shape[dim + 1], *shape[dim + 2 :])


def gathered_copies(x, axis, dim):
    parts = from_everyone(x, axis)
    return joined_along(parts, dim)


def in_blocks(x, dim, size):
    before, after = (x.shape[:dim], x.shape[dim + 1 :])
    return jnp.moveaxis(x.reshape(*before, size, -1, *after), dim, 0)


def sent_and_summed(x, axis, dim):
    size = lax.axis_size(axis)
    parts = lax.all_to_all(in_blocks(x, dim, size), axis, 0, 0, tiled=True)
    return jnp.sum(parts, axis=0)


def from_behind(value, axis, steps):
    count = lax.axis_size(axis)
    leading, last = (max(0, -steps), min(count, count - steps))
    return lax.ppermute(value, axis, [(source, source + steps) for source in range(leading, last)])


def pack_rows(position, shape, corr, dest, cell, sub_count):
    owner = dest // sub_count
    row = owner * BAND + cell // NCOL
    column = cell % NCOL
    axis_x = shape[0]
    axis_y = shape[1]
    return jnp.stack(
        [
            position[0],
            position[1],
            axis_x * axis_x,
            axis_y * axis_y,
            corr * axis_x * axis_y,
            row.astype(jnp.float32) + row_offset,
            column.astype(jnp.float32),
        ]
    )


def empty_rows(width, code):
    base = jnp.zeros((7, width), jnp.float32)
    return base.at[2:4].set(1.0).at[5].set(code)


def pair_terms(gaia, wise):
    row_gap = gaia[5][:, None] - wise[5][None, :]
    col_gap = jnp.mod(gaia[6][:, None] - wise[6][None, :] + 1.0, NCOL) - 1.0
    near = (jnp.abs(row_gap) <= 1.0) & (jnp.abs(col_gap) <= 1.0)
    step_x = col_gap + gaia[0][:, None] - wise[0][None, :]
    step_y = row_gap + gaia[1][:, None] - wise[1][None, :]
    spread_x = gaia[2][:, None] + wise[2][None, :]
    spread_y = gaia[3][:, None] + wise[3][None, :]
    spread_xy = gaia[4][:, None] + wise[4][None, :]
    determinant = spread_x * spread_y - spread_xy * spread_xy
    chi_square = (
        spread_y * step_x * step_x - 2.0 * spread_xy * step_x * step_y + spread_x * step_y * step_y
    ) / determinant
    like = jnp.where(near, jnp.exp(-0.5 * chi_square) * inv_two_pi / jnp.sqrt(determinant), 0.0)
    return (
        jnp.sum(like, axis=1),
        jnp.sum(like * step_x, axis=1),
        jnp.sum(like * step_y, axis=1),
        jnp.sum(like, axis=0),
    )


def slots_of(dest, capacity):
    order = jnp.arange(dest.shape[0], dtype=jnp.int32)
    same = (dest[:, None] == dest[None, :]) & (order[None, :] < order[:, None])
    rank = jnp.sum(same.astype(jnp.int32), axis=1, dtype=jnp.int32)
    return dest * capacity + rank


def fold_columns(rows, block_width, carry, piece):
    row_totals, column_totals = carry
    count = piece.shape[1]
    blocks = piece.reshape(7, count // block_width, block_width).transpose(1, 0, 2)

    def column_step(totals, part):
        like, moment_x, moment_y, column_sums = pair_terms(rows, part)
        return (totals + jnp.stack([like, moment_x, moment_y]), column_sums)

    row_totals, column_sums = lax.scan(column_step, row_totals, blocks)
    column_totals = column_sums.reshape(-1)
    return (row_totals, column_totals)


def shards(
    gaia_pos,
    gaia_shape,
    gaia_corr,
    gaia_dest,
    gaia_cell,
    wise_pos,
    wise_shape,
    wise_corr,
    wise_dest,
    wise_cell,
):
    pix_count = lax.axis_size("pix")
    sub_count = lax.axis_size("sub")
    targets = pix_count * sub_count
    capacity = max(2, 5 * SRC_DEV // (2 * targets))
    received = targets * capacity
    block_width = received // 2
    gaia_rows = pack_rows(gaia_pos, gaia_shape, gaia_corr, gaia_dest[:, 0], gaia_cell, sub_count)
    wise_rows = pack_rows(wise_pos, wise_shape, wise_corr, wise_dest[:, 0], wise_cell, sub_count)
    gaia_slot = slots_of(gaia_dest[:, 0], capacity)
    wise_slot = slots_of(wise_dest[:, 0], capacity)
    gaia_send = empty_rows(received, empty_gaia).at[:, gaia_slot].set(gaia_rows)
    wise_send = empty_rows(received, empty_wise).at[:, wise_slot].set(wise_rows)
    gaia_here, wise_here = side_by_side((gaia_send, wise_send), ("pix", "sub"), 1, 1, 0)
    nearby = with_halo(wise_here, (("pix", 1),), received)
    members = sub_count * lax.axis_size("rep")
    start_totals = (
        jnp.zeros((3, received), jnp.float32),
        jnp.zeros((members * 3 * received,), jnp.float32),
    )
    gaia_result, column_totals = fold_columns(
        gaia_here, block_width, start_totals, gathered_copies(nearby, ("sub", "rep"), 1)
    )
    wise_part = sent_and_summed(column_totals, ("sub", "rep"), 0)
    from_upper = from_behind(wise_part[:received], "pix", -1)
    from_lower = from_behind(wise_part[2 * received :], "pix", 1)
    wise_result = wise_part[received : 2 * received] + from_lower + from_upper
    results = jnp.concatenate([gaia_result, wise_result[None, :]], axis=0)
    returned = lax.all_to_all(results, ("pix", "sub"), split_axis=1, concat_axis=1, tiled=True)
    return (returned[0][gaia_slot], returned[1:3][:, gaia_slot], returned[3][wise_slot])


def solution(mesh):
    return jax.shard_map(
        shards,
        mesh=mesh,
        in_specs=(
            P(None, ("groups", "pix", "sub", "rep")),
            P(None, ("groups", "pix", "sub", "rep")),
            P(("groups", "pix", "sub", "rep")),
            P(("groups", "pix", "sub", "rep"), None),
            P(("groups", "pix", "sub", "rep")),
            P(None, ("groups", "pix", "sub", "rep")),
            P(None, ("groups", "pix", "sub", "rep")),
            P(("groups", "pix", "sub", "rep")),
            P(("groups", "pix", "sub", "rep"), None),
            P(("groups", "pix", "sub", "rep")),
        ),
        out_specs=(
            P(("groups", "pix", "sub", "rep")),
            P(None, ("groups", "pix", "sub", "rep")),
            P(("groups", "pix", "sub", "rep")),
        ),
        check_vma=False,
    )
```

profile of v0, /device:TPU:40, one launch (start us, length us, event | category | flops | bytes accessed | tf_op | source)
XLA Modules:
  0.0 202.0 jit_solution(5425317804277985309)
XLA Ops:
  0.6 0.6 copy-done.6
  1.5 0.7 copy-done.2
  2.2 0.6 copy-done.8
  2.8 0.6 copy-done.7
  3.5 0.7 copy-done.4
  4.4 0.6 copy-done.9
  5.4 1.0 scatter_fusion.1
  6.4 1.0 scatter_fusion
  7.4 79.9 %all_to_all.29 = f32[14,128,2]{0,2,1:T(2,128)S(1)} all-to-all(f32[14,128,2]{0,2,1:T(2,128)S(1)} %bitcast.106), channel_id=1, replica_groups=mesh['groups'=2,'pix'=32,'sub'=4,'rep'=2] {'pix','sub'}, dimensions={1} | all-to-all | bytes 28672 | tf_op jit(solution)/shard_map/all_to_all | solution.py:25
  87.5 1.3 collective-permute-start.1
  88.8 5.2 %collective-permute-start = (f32[7,256]{0,1:T(8,128)S(1)}, f32[7,256]{0,1:T(8,128)S(1)}, u32[]{:S(2)}, u32[]{:S(2)}) collective-permute-start(f32[7,256]{0,1:T(8,128)S(1)} %bitcast.109), channel_id=1, source_target_pairs={{0,8},{8,16},{16,24},{24,32},{32,40},{40,48},{48,56},{56,64},{64,7... | collective-permute-start | bytes 21512 | tf_op jit(solution)/shard_map/ppermute | solution.py:39
  94.1 0.9 collective-permute-done.1
  95.1 1.5 collective-permute-done
  96.6 0.7 broadcast_in_dim.16
  97.3 4.5 %all-to-all-start.1 = ((f32[8,7,768]{2,1,0:T(8,128)}), f32[8,7,768]{2,1,0:T(8,128)S(1)}, u32[]{:S(2)}, u32[]{:S(2)}) async-start(f32[8,7,768]{2,1,0:T(8,128)} %broadcast_in_dim.16), calls=%async_computation.1 | async-start | bytes 393216 | tf_op jit(solution)/shard_map/all_to_all | solution.py:47
  101.9 6.7 %all-to-all-done.1 = f32[8,7,768]{2,1,0:T(8,128)S(1)} async-done(((f32[8,7,768]{2,1,0:T(8,128)}), f32[8,7,768]{2,1,0:T(8,128)S(1)}, u32[]{:S(2)}, u32[]{:S(2)}) %all-to-all-start.1) | async-done | bytes 172064 | tf_op jit(solution)/shard_map/all_to_all | solution.py:47
  108.6 29.2 %while.19 = (s32[]{:T(128)}, f32[3,256]{1,0:T(4,128)S(1)}, f32[48,128]{1,0:T(8,128)S(1)}, f32[7,256]{1,0:T(8,128)S(1)}, f32[48,7,128]{2,1,0:T(8,128)S(1)}, /*index=5*/s32[]{:T(128)}, s32[]{:T(128)}) while((s32[]{:T(128)}, f32[3,256]{1,0:T(4,128)S(1)}, f32[48,128]{1,0:T(8,128)S(1)}, f32[7,256]{1,0:T(8,128)S(1)}, ...), condition=%wide.region_9.10_spmd.clone, body=%wide.region_4.0_spmd.clone.sunk | while | flops 1476739 | bytes 53351 | solution.py:140
  108.6 0.5 fusion.39
  109.3 0.5 fusion.39
  109.9 0.5 fusion.39
  110.5 0.5 fusion.39
  111.1 0.5 fusion.39
  111.7 0.5 fusion.39
  112.3 0.5 fusion.39
  112.9 0.5 fusion.39
  113.5 0.5 fusion.39
  114.1 0.5 fusion.39
  114.7 0.5 fusion.39
  115.3 0.5 fusion.39
  116.0 0.5 fusion.39
  116.6 0.5 fusion.39
  117.2 0.5 fusion.39
  117.8 0.5 fusion.39
  118.4 0.5 fusion.39
  119.0 0.5 fusion.39
  119.6 0.5 fusion.39
  137.8 7.8 %all_to_all.30 = f32[8,1,768]{2,1,0:T(1,128)S(1)} all-to-all(f32[8,1,768]{2,1,0:T(1,128)S(1)} %bitcast.124), channel_id=1, replica_groups=mesh['groups'=2,'pix'=32,'sub'=4,'rep'=2] {'sub','rep'}, dimensions={0} | all-to-all | bytes 49152 | tf_op jit(solution)/shard_map/all_to_all | solution.py:68
  145.7 1.3 collective-permute-start.3
  147.0 5.0 %collective-permute-start.2 = (f32[256]{0:T(256)S(1)}, f32[256]{0:T(256)S(1)}, u32[]{:S(2)}, u32[]{:S(2)}) collective-permute-start(f32[256]{0:T(256)S(1)} %get-tuple-element.202), channel_id=1, source_target_pairs={{0,8},{8,16},{16,24},{24,32},{32,40},{40,48},{48,56},{56,64},{64,7... | collective-permute-start | bytes 3080 | tf_op jit(solution)/shard_map/ppermute | solution.py:75
  152.3 1.1 collective-permute-done.2
  153.5 1.5 copy.55
  155.0 15.4 %all-to-all-start.3 = ((f32[4,128,2]{0,2,1:T(2,128)}), f32[4,128,2]{0,2,1:T(2,128)S(1)}, u32[]{:S(2)}, u32[]{:S(2)}) async-start(f32[4,128,2]{0,2,1:T(2,128)} %copy.55), calls=%async_computation.3 | async-start | bytes 262144 | tf_op jit(solution)/shard_map/all_to_all | solution.py:184
  170.4 25.8 %all-to-all-done.3 = f32[4,128,2]{0,2,1:T(2,128)S(1)} async-done(((f32[4,128,2]{0,2,1:T(2,128)}), f32[4,128,2]{0,2,1:T(2,128)S(1)}, u32[]{:S(2)}, u32[]{:S(2)}) %all-to-all-start.3) | async-done | bytes 4128 | tf_op jit(solution)/shard_map/all_to_all | solution.py:184
  196.2 0.5 slice_reduce_fusion
  196.9 1.8 gather_fusion
  198.9 0.6 gather_fusion.1
  199.5 0.6 copy.56
  200.3 1.8 gather_fusion.2
  (322 shorter events, 20.2 us)
Async XLA Ops:
  0.6 0.7 copy-start.6
  1.5 0.7 copy-start.2
  2.1 0.7 copy-start.8
  2.8 0.7 copy-start.7
  3.5 0.7 copy-start.4
  4.3 0.7 copy-start.9
  4.3 0.8 copy-start.3
  4.3 0.8 copy-start.11
  4.3 0.9 copy-start.10
  4.3 0.9 copy-start.5
  4.4 1.0 copy-start
  4.4 2.0 copy-start.1
  87.5 7.5 %collective-permute-start.1 = (f32[7,256]{0,1:T(8,128)S(1)}, f32[7,256]{0,1:T(8,128)S(1)}, u32[]{:S(2)}, u32[]{:S(2)}) collective-permute-start(f32[7,256]{0,1:T(8,128)S(1)} %bitcast.108), channel_id=1, source_target_pairs={{8,0},{16,8},{24,16},{32,24},{40,32},{48,40},{56,48},{64,56},{72,6... | collective-permute-start | bytes 21512 | tf_op jit(solution)/shard_map/ppermute | solution.py:40
  88.8 7.7 %collective-permute-start = (f32[7,256]{0,1:T(8,128)S(1)}, f32[7,256]{0,1:T(8,128)S(1)}, u32[]{:S(2)}, u32[]{:S(2)}) collective-permute-start(f32[7,256]{0,1:T(8,128)S(1)} %bitcast.109), channel_id=1, source_target_pairs={{0,8},{8,16},{16,24},{24,32},{32,40},{40,48},{48,56},{56,64},{64,7... | collective-permute-start | bytes 21512 | tf_op jit(solution)/shard_map/ppermute | solution.py:39
  97.3 11.3 %all-to-all-start.1 = ((f32[8,7,768]{2,1,0:T(8,128)}), f32[8,7,768]{2,1,0:T(8,128)S(1)}, u32[]{:S(2)}, u32[]{:S(2)}) async-start(f32[8,7,768]{2,1,0:T(8,128)} %broadcast_in_dim.16), calls=%async_computation.1 | async-start | bytes 393216 | tf_op jit(solution)/shard_map/all_to_all | solution.py:47
  145.7 6.5 %collective-permute-start.3 = (f32[256]{0:T(256)S(1)}, f32[256]{0:T(256)S(1)}, u32[]{:S(2)}, u32[]{:S(2)}) collective-permute-start(f32[256]{0:T(256)S(1)} %get-tuple-element.203), channel_id=1, source_target_pairs={{8,0},{16,8},{24,16},{32,24},{40,32},{48,40},{56,48},{64,56},{72,6... | collective-permute-start | bytes 3080 | tf_op jit(solution)/shard_map/ppermute | solution.py:75
  147.0 6.3 %collective-permute-start.2 = (f32[256]{0:T(256)S(1)}, f32[256]{0:T(256)S(1)}, u32[]{:S(2)}, u32[]{:S(2)}) collective-permute-start(f32[256]{0:T(256)S(1)} %get-tuple-element.202), channel_id=1, source_target_pairs={{0,8},{8,16},{16,24},{24,32},{32,40},{40,48},{48,56},{56,64},{64,7... | collective-permute-start | bytes 3080 | tf_op jit(solution)/shard_map/ppermute | solution.py:75
  155.0 41.2 %all-to-all-start.3 = ((f32[4,128,2]{0,2,1:T(2,128)}), f32[4,128,2]{0,2,1:T(2,128)S(1)}, u32[]{:S(2)}, u32[]{:S(2)}) async-start(f32[4,128,2]{0,2,1:T(2,128)} %copy.55), calls=%async_computation.3 | async-start | bytes 262144 | tf_op jit(solution)/shard_map/all_to_all | solution.py:184
where the time goes:
time: 203 us; the launch traced here: 202 us
  blocking collectives  87.7 us (43%)
  waiting for transfers between devices  36 us (18%)
  starting transfers between devices  32.7 us (16%)
  other arithmetic  25 us (12%)
  local copies, waits for them, and re-layouts  17.8 us (9%)
    all_to_all x1, blocking collectives, side_by_side(): lax.all_to_all(both, axis, split_axis=split_dim, concat_axis=concat_dim,...  79.9 us
    all_to_all x1, waiting for transfers between devices, shards(): lax.all_to_all(results, ('pix', 'sub'), split_axis=1, concat_axis=1, tile...  25.8 us
    reduce_sum x48, other arithmetic, pair_terms(): jnp.sum(like, axis=0)  23.5 us
    all_to_all x1, starting transfers between devices, shards(): lax.all_to_all(results, ('pix', 'sub'), split_axis=1, concat_axis=1, tile...  15.4 us
    all_to_all x1, blocking collectives, sent_and_summed(): parts = lax.all_to_all(in_blocks(x, dim, size), axis, 0, 0, tiled=True)  7.82 us
    all_to_all x1, waiting for transfers between devices, from_everyone(): lax.all_to_all(jnp.broadcast_to(x[None], (size, *x.shape)), axis, 0, 0, t...  6.72 us
    ppermute x2, starting transfers between devices, from_behind(): lax.ppermute(value, axis, [(source, source + steps) for source in range(l...  6.33 us
    ppermute x1, starting transfers between devices, with_halo(): before = lax.ppermute(last, axis, up)  5.24 us
  transfers between devices with their start and end apart: 6, of which 5 were waited for; matrix products, arithmetic and copies ran while one was open for 0% of the time, Pallas kernels for 0%

commit v1 on v0

v1 whole, which is shorter than its diff:
```python
import math

import jax
import jax.numpy as jnp
from jax import lax
from jax.experimental import pallas as pl
from jax.experimental.pallas import tpu as pltpu
from jax.sharding import PartitionSpec as P

NCOL = 64
CAP = 2
LANES = 128
SLOT_LANES = 16
FIELDS = 8
EMPTY_BIT = 4096
ROW_BIT = 8192
LAMBDA = 2.0 * math.log(2.0)
GAIN = LAMBDA / (2.0 * math.pi)
GROUPS = 4
USED = 6
INTERPRET = False

f32 = jnp.float32
bf16 = jnp.bfloat16
i32 = jnp.int32


def iota(shape, dim):
    return lax.broadcasted_iota(i32, shape, dim)


def split3(x):
    high = x.astype(bf16)
    rest = x - high.astype(f32)
    middle = rest.astype(bf16)
    low = (rest - middle.astype(f32)).astype(bf16)
    return high, middle, low


def dot(a, b, contract):
    return lax.dot_general(a, b, (contract, ((), ())), preferred_element_type=f32)


def one_hot(mask):
    return jnp.where(mask, 1.0, 0.0).astype(bf16)


def call(body, outs, scratch=()):
    return pl.pallas_call(
        body,
        out_shape=outs,
        scratch_shapes=list(scratch),
        compiler_params=pltpu.CompilerParams(vmem_limit_bytes=8 << 20),
        interpret=INTERPRET,
    )


def owners_and_ranks(dest_g, dest_w, sub_count):
    n = dest_g.shape[1]
    shift = sub_count.bit_length() - 1
    own_g, own_w = dest_g >> shift, dest_w >> shift
    both = jnp.concatenate([own_g.astype(f32), own_w.astype(f32), jnp.zeros((6, n), f32)], axis=0)
    columns = jnp.transpose(both)
    earlier = iota((n, n), 0) < iota((n, n), 1)

    def rank(row, column):
        same = (row.astype(f32) == column) & earlier
        return jnp.sum(jnp.where(same, 1.0, 0.0), axis=0, keepdims=True).astype(i32)

    return own_g, own_w, rank(own_g, columns[:, 0:1]), rank(own_w, columns[:, 1:2])


def send_body(pix_count, sub_count):
    slots = CAP * sub_count

    def body(gp, gs, gc, gd, gl, wp, ws, wc, wd, wl, msg):
        n = gp.shape[1]
        own_g, own_w, rank_g, rank_w = owners_and_ranks(gd[...], wd[...], sub_count)

        def fields(pos, shape, corr, cell):
            a, b = shape[0:1, :], shape[1:2, :]
            return jnp.concatenate(
                [
                    pos[0:1, :],
                    pos[1:2, :],
                    (a * a) * LAMBDA,
                    (b * b) * LAMBDA,
                    ((corr * a) * b) * (2.0 * LAMBDA),
                    cell.astype(f32) + 1.0,
                    jnp.zeros((2, n), f32),
                ],
                axis=0,
            )

        data_g = fields(gp, gs, gc[...], gl[...])
        data_w = fields(wp, ws, wc[...], wl[...])
        zero = jnp.zeros((FIELDS, n), f32)
        left, right = [], []
        for s in range(slots):
            left += [jnp.where(rank_g == s, data_g, 0.0), zero]
            right += [zero, jnp.where(rank_w == s, data_w, 0.0)]
        table = jnp.concatenate([jnp.concatenate(left, axis=0), jnp.concatenate(right, axis=0)], axis=1)
        rows = 3 * pix_count
        r = iota((rows, 2 * n), 0)
        target = jnp.floor((r.astype(f32) + 0.5) * (1.0 / 3.0)).astype(i32)
        side = r - 3 * target
        owner = jnp.concatenate([own_g, own_w], axis=1)
        upper = jnp.concatenate([gl[...], wl[...]], axis=1) >> (NCOL.bit_length() - 1)
        wanted = (owner == target + side - 1) & ((side == 1) | (upper == jnp.where(side == 0, 1, 0)))
        pick = one_hot(wanted)
        msg[...] = sum(dot(pick, part, ((1,), (1,))) for part in split3(table))

    return body


def compact_body(pix_count, slots, members, width):
    own_lanes = pix_count

    def body(got, out, own, ranks, chunk):
        lanes = 3 * pix_count
        parts = [got[pl.ds(j, pix_count, stride=3), :] for j in (1, 0, 2)]
        parts.append(jnp.zeros((LANES - lanes, LANES), f32))
        data = jnp.transpose(jnp.concatenate(parts, axis=0))
        lane8 = iota((FIELDS, LANES), 1)
        row8 = iota((FIELDS, LANES), 0)
        is_own = lane8 < own_lanes
        is_low = (lane8 >= own_lanes) & (lane8 < 2 * own_lanes)
        before = one_hot(iota((LANES, LANES), 0) < iota((LANES, LANES), 1))
        below = one_hot(iota((slots, slots), 1) < iota((slots, slots), 0))
        chunk[...] = jnp.zeros(chunk.shape, f32)
        rank_rows = []
        for c in range(2):
            pieces, codes = [], []
            for s in range(slots):
                x = data[s * SLOT_LANES + c * FIELDS : s * SLOT_LANES + (c + 1) * FIELDS, :]
                code = x[5:6, :]
                filled = code > 0.5
                cell = code.astype(i32) - 1
                row = jnp.where(is_own, cell >> 6, jnp.where(is_low, -1, 2)).astype(f32)
                away = jnp.where(is_own, 0, jnp.where(is_low, 512, 256))
                own_row = jnp.where(is_own, (cell >> 6) * ROW_BIT, 0)
                seen = ((cell & (NCOL - 1)) - away + EMPTY_BIT + own_row).astype(f32)
                x = jnp.where(row8 == 1, x + row, jnp.where(row8 == 5, seen, x))
                pieces.append(jnp.where(filled, x, 0.0))
                codes.append(code)
            filled = jnp.concatenate(codes, axis=0) > 0.5
            flag_own = jnp.where(filled & (iota((slots, LANES), 1) < own_lanes), 1.0, 0.0)
            flag_far = jnp.where(filled & (iota((slots, LANES), 1) >= own_lanes), 1.0, 0.0)

            def places(flag):
                inside = dot(flag.astype(bf16), before, ((1,), (0,)))
                totals = jnp.broadcast_to(jnp.sum(flag, axis=1, keepdims=True), (slots, LANES))
                ahead = dot(below, totals.astype(bf16), ((1,), (0,)))
                return inside + ahead, jnp.sum(totals, axis=0, keepdims=True)

            place_own, count_own = places(flag_own)
            place_far, count_far = places(flag_far)
            place = jnp.where(flag_own > 0.5, place_own, place_far + count_own)
            place = jnp.where(filled, place, -1.0)
            count = count_own + count_far
            rank_rows.append(place)
            stacked = [jnp.concatenate(split3(p), axis=0) for p in pieces]
            total = jnp.max(count)
            for t in range(width // LANES):

                @pl.when(total > t * LANES)
                def _(t=t, c=c, place=place, stacked=stacked, count=count, count_own=count_own):
                    goal = iota((LANES, LANES), 0).astype(f32) + float(t * LANES)
                    acc = jnp.zeros((3 * FIELDS, LANES), f32)
                    for s in range(slots):
                        pick = one_hot(goal == place[s : s + 1, :])
                        acc = acc + dot(stacked[s], pick, ((1,), (1,)))
                    x = acc[0:8, :] + acc[8:16, :] + acc[16:24, :]
                    x = jnp.where(row8 == 6, count, jnp.where(row8 == 7, count_own, x))
                    chunk[c * FIELDS : (c + 1) * FIELDS, t * LANES : (t + 1) * LANES] = x

        ranks[...] = jnp.transpose(jnp.concatenate(rank_rows + [jnp.zeros((LANES - 2 * slots, LANES), f32)], axis=0))
        value = chunk[...]
        own[...] = value[:, : own.shape[1]]
        for d in range(members):
            out[d] = value

    return body


def match_body(pix_count, slots, members, width):
    block = 8 * GROUPS
    used = 2 * USED
    early = 5 * block

    def body(near, own, ranks, out, wide, line, totals):
        own_width = pix_count * slots
        lane8 = iota((8, LANES), 1)
        stacked = jnp.concatenate([p.astype(f32) for p in split3(own[...])], axis=0)
        columns = jnp.transpose(stacked).astype(bf16)
        spread_to = iota((6 * FIELDS, used * LANES), 1) >> 7
        field_of = spread_to + jnp.where(spread_to >= USED, FIELDS - USED, 0)
        spread = one_hot((iota((6 * FIELDS, used * LANES), 0) & (2 * FIELDS - 1)) == field_of)
        wide[0:early, :] = dot(columns[0:early, :], spread, ((1,), (0,)))
        count_own = [jnp.max(own[c * FIELDS + 7 : c * FIELDS + 8, 0:LANES]).astype(i32) for c in range(2)]

        @pl.when(jnp.maximum(count_own[0], count_own[1]) > early)
        def _():
            wide[early:own_width, :] = dot(columns[early:own_width, :], spread, ((1,), (0,)))

        counts = [
            [jnp.max(near[d, c * FIELDS + 6 : c * FIELDS + 7, 0:LANES]).astype(i32) for d in range(members)] for c in range(2)
        ]
        ends = []
        for c in range(2):
            start = jnp.int32(0)
            for d in range(members):
                shift = start & (LANES - 1)
                base = start >> 7
                keep = lane8 >= shift

                def put(k, x, c=c, base=base):
                    line[c, base + k] = x

                def turned(k, c=c, d=d, shift=shift):
                    return pltpu.roll(near[d, c * FIELDS : (c + 1) * FIELDS, k * LANES : (k + 1) * LANES], shift, 1)

                last = jnp.zeros((FIELDS, LANES), f32) if d == 0 else line[c, base]
                for k in range(3):
                    now = turned(k)
                    put(k, jnp.where(keep, now, last))
                    last = now
                put(3, jnp.where(keep, 0.0, last))
                put(4, jnp.zeros((FIELDS, LANES), f32))

                @pl.when(counts[c][d] > 3 * LANES)
                def _(c=c, base=base, keep=keep, put=put, turned=turned):
                    last = line[c, base + 3]
                    for k in range(3, width // LANES):
                        now = turned(k)
                        put(k, jnp.where(keep, now, last))
                        last = now
                    put(width // LANES, jnp.where(keep, 0.0, last))
                    put(width // LANES + 1, jnp.zeros((FIELDS, LANES), f32))

                start = start + counts[c][d]
            ends.append(lax.div(start + (2 * LANES - 1), 2 * LANES))

        for c in range(2):
            other = 1 - c
            blocks = lax.div(count_own[c] + (block - 1), block)

            def own_block(b, _, c=c, other=other):
                base = pl.multiple_of(b * block, 8)
                fields = []
                for g in range(GROUPS):
                    col = [wide[pl.ds(base + 8 * g, 8), (c * USED + f) * LANES : (c * USED + f + 1) * LANES] for f in range(USED)]
                    code = col[5].astype(i32)
                    own_code = code + (NCOL + 1 - EMPTY_BIT)
                    mask = jnp.where(code < ROW_BIT, 256, 512) | (EMPTY_BIT | (NCOL - 1))
                    fields.append((col[0] - 1.0, col[1], col[2], col[3], col[4], own_code, mask))

                def pairs(t, acc):
                    acc = [list(a) for a in acc]
                    for half in range(2):
                        at = line.at[other, 2 * t + half]
                        row = [jnp.broadcast_to(at[f : f + 1, :], (8, LANES)) for f in range(USED)]
                        code = row[5].astype(i32) - EMPTY_BIT
                        for g in range(GROUPS):
                            px, py, xx, yy, xy, own_code, mask = fields[g]
                            step = (own_code - code) & mask
                            dx = step.astype(f32) + (px - row[0])
                            dy = py - row[1]
                            sx, sy, sxy = xx + row[2], yy + row[3], xy + row[4]
                            det = sx * sy - 0.25 * (sxy * sxy)
                            root = lax.rsqrt(det)
                            chi = dy * (sxy * dx - sx * dy) - sy * (dx * dx)
                            like = jnp.exp2(chi * (root * root)) * root
                            like = jnp.where(step <= 2, like, 0.0)
                            acc[g][0] = acc[g][0] + like
                            if c == 0:
                                acc[g][1] = acc[g][1] + like * dx
                                acc[g][2] = acc[g][2] + like * dy
                    return tuple(tuple(a) for a in acc)

                zero = jnp.zeros((8, LANES), f32)
                acc = tuple((zero,) * (3 if c == 0 else 1) for _ in range(GROUPS))
                acc = lax.fori_loop(0, ends[other], pairs, acc)
                for g in range(GROUPS):
                    for k, a in enumerate(acc[g]):
                        totals[3 * c + k, pl.ds(base + 8 * g, 8), :] = a
                return 0

            lax.fori_loop(0, blocks, own_block, 0)

        f_of_lane = lane8 & (SLOT_LANES - 1)
        goal = iota((pix_count, own_width), 1).astype(f32)
        picks, values = [], []
        for c in range(2):
            columns = [ranks[0:pix_count, c * slots + s : c * slots + s + 1] for s in range(slots)]
            picks.append(jnp.concatenate([one_hot(r == goal) for r in columns], axis=0))
            rows = []
            for g in range(own_width // 8):
                live = (iota((8, LANES), 0) + 8 * g) < count_own[c]
                value = jnp.zeros((8, LANES), f32)
                for k in range(3 if c == 0 else 1):
                    total = jnp.sum(totals[3 * c + k, 8 * g : 8 * g + 8, :], axis=1, keepdims=True) * GAIN
                    value = jnp.where(f_of_lane == c * FIELDS + k, total, value)
                rows.append(jnp.where(live, value, 0.0))
            values.append(jnp.concatenate(rows, axis=0))
        pick = jnp.concatenate(picks, axis=1)
        result = sum(dot(pick, part, ((1,), (0,))) for part in split3(jnp.concatenate(values, axis=0)))
        slot_of_lane = iota((pix_count, LANES), 1) >> 4
        final = jnp.zeros((pix_count, LANES), f32)
        for s in range(slots):
            final = final + jnp.where(slot_of_lane == s, result[s * pix_count : (s + 1) * pix_count, :], 0.0)
        out[...] = final

    return body


def return_body(pix_count, sub_count):
    slots = CAP * sub_count

    def body(back, gd, wd, like, offset, wise):
        n = gd.shape[1]
        own_g, own_w, rank_g, rank_w = owners_and_ranks(gd[...], wd[...], sub_count)
        owner = jnp.concatenate([own_g, own_w], axis=1)
        pick = one_hot(iota((pix_count, 2 * n), 0) == owner)
        turned = jnp.transpose(back[...])
        found = sum(dot(part, pick, ((1,), (0,))) for part in split3(turned))
        gaia = jnp.zeros((FIELDS, n), f32)
        other = jnp.zeros((FIELDS, n), f32)
        for s in range(slots):
            at = s * SLOT_LANES
            gaia = gaia + jnp.where(rank_g == s, found[at : at + FIELDS, 0:n], 0.0)
            other = other + jnp.where(rank_w == s, found[at + FIELDS : at + 2 * FIELDS, n : 2 * n], 0.0)
        like[...] = gaia[0:1, :]
        offset[...] = gaia[1:3, :]
        wise[...] = other[0:1, :]

    return body


def stages(pix_count, sub_count, members, n):
    slots = CAP * sub_count
    width = 3 * pix_count * slots
    own_width = pix_count * slots
    send = call(send_body(pix_count, sub_count), jax.ShapeDtypeStruct((3 * pix_count, LANES), f32))
    compact = call(
        compact_body(pix_count, slots, members, width),
        (
            jax.ShapeDtypeStruct((members, 2 * FIELDS, width), f32),
            jax.ShapeDtypeStruct((2 * FIELDS, own_width), f32),
            jax.ShapeDtypeStruct((LANES, LANES), f32),
        ),
        [pltpu.VMEM((2 * FIELDS, width), f32)],
    )
    match = call(
        match_body(pix_count, slots, members, width),
        jax.ShapeDtypeStruct((pix_count, LANES), f32),
        [
            pltpu.VMEM((own_width, 2 * USED * LANES), f32),
            pltpu.VMEM((2, members * width // LANES + 8, FIELDS, LANES), f32),
            pltpu.VMEM((4, own_width, LANES), f32),
        ],
    )
    back = call(
        return_body(pix_count, sub_count),
        (
            jax.ShapeDtypeStruct((1, n), f32),
            jax.ShapeDtypeStruct((2, n), f32),
            jax.ShapeDtypeStruct((1, n), f32),
        ),
    )
    return send, compact, match, back


def shards(gaia_pos, gaia_shape, gaia_corr, gaia_dest, gaia_cell, wise_pos, wise_shape, wise_corr, wise_dest, wise_cell):
    pix_count = lax.axis_size("pix")
    sub_count = lax.axis_size("sub")
    members = sub_count * lax.axis_size("rep")
    n = gaia_pos.shape[1]
    send, compact, match, back = stages(pix_count, sub_count, members, n)
    row = lambda x: x.reshape(1, n)
    gd, wd = row(gaia_dest), row(wise_dest)
    msg = send(gaia_pos, gaia_shape, row(gaia_corr), gd, row(gaia_cell), wise_pos, wise_shape, row(wise_corr), wd, row(wise_cell))
    got = lax.all_to_all(msg.reshape(pix_count, 1, 3 * LANES), "pix", 0, 0, tiled=True)
    chunks, own, ranks = compact(got.reshape(3 * pix_count, LANES))
    near = lax.all_to_all(chunks, ("sub", "rep"), 0, 0, tiled=True)
    results = match(near, own, ranks)
    returned = lax.all_to_all(results.reshape(pix_count, 1, LANES), "pix", 0, 0, tiled=True)
    like, offset, wise = back(returned.reshape(pix_count, LANES), gd, wd)
    return like.reshape(n), offset, wise.reshape(n)


def solution(mesh):
    flat = P(("groups", "pix", "sub", "rep"))
    pair = P(None, ("groups", "pix", "sub", "rep"))
    column = P(("groups", "pix", "sub", "rep"), None)
    return jax.shard_map(
        shards,
        mesh=mesh,
        in_specs=(pair, pair, flat, column, flat, pair, pair, flat, column, flat),
        out_specs=(flat, pair, flat),
        check_vma=False,
    )
```

time: 203 us -> 120 us (0.59)
  waiting for transfers between devices: 36 us -> 0 us
  starting transfers between devices: 32.7 us -> 0 us
  other arithmetic: 25 us -> 0 us
  blocking collectives: 87.7 us -> 108 us
  local copies, waits for them, and re-layouts: 17.8 us -> 0.71 us
  Pallas kernels: 0 us -> 9.52 us
    all_to_all x2 -> x0, waiting for transfers between devices: 32.5 us -> none  [the longest x1 25.8 us: shards(): lax.all_to_all(results, ('pix', 'sub'), split_axis=1, concat_axis=1, tile...]
    reduce_sum x51 -> x0, other arithmetic: 23.9 us -> none  [the longest x48 23.5 us: pair_terms(): jnp.sum(like, axis=0)]
    all_to_all x2 -> x3, blocking collectives: 87.7 us -> 108 us  [the longest x1 69.5 us: shards(): lax.all_to_all(msg.reshape(pix_count, 1, 3 * LANES), 'pix', 0, 0, tiled=T...]
    all_to_all x2 -> x0, starting transfers between devices: 19.9 us -> none  [the longest x1 15.4 us: shards(): lax.all_to_all(results, ('pix', 'sub'), split_axis=1, concat_axis=1, tile...]
    ppermute x4 -> x0, starting transfers between devices: 12.9 us -> none  [the longest x2 6.33 us: from_behind(): lax.ppermute(value, axis, [(source, source + steps) for source in range(l...]
    pallas_call x0 -> x4, Pallas kernels: none -> 9.52 us  [the longest x1 6.62 us: shards(): results = match(near, own, ranks)]
    gather x3 -> x0, local copies, waits for them, and re-layouts: 4.18 us -> none  [the longest x1 1.77 us: shards(): returned[0][gaia_slot]]
    unnamed x26 -> x20, local copies, waits for them, and re-layouts: 4.61 us -> 0.71 us
  transfers between devices with their start and end apart: 6 -> 0, of which waited for: 5 -> 0; matrix products, arithmetic and copies ran while one was open for 0% -> 0% of each run, Pallas kernels for 0% -> 0%
where the time goes in v1:
time: 120 us; the launch traced here: 119 us
  blocking collectives  108 us (90%)
  Pallas kernels  9.52 us (8%)
    all_to_all x1, blocking collectives, shards(): lax.all_to_all(msg.reshape(pix_count, 1, 3 * LANES), 'pix', 0, 0, tiled=T...  69.5 us
    all_to_all x1, blocking collectives, shards(): lax.all_to_all(results.reshape(pix_count, 1, LANES), 'pix', 0, 0, tiled=T...  25.3 us
    all_to_all x1, blocking collectives, shards(): near = lax.all_to_all(chunks, ('sub', 'rep'), 0, 0, tiled=True)  13.6 us
    pallas_call x1, Pallas kernels, shards(): results = match(near, own, ranks)  6.62 us

profile of v1, /device:TPU:40, one launch (start us, length us, event | category | flops | bytes accessed | tf_op | source)
XLA Modules:
  0.0 119.3 jit_solution(12900930025460619253)
XLA Ops:
  0.6 0.0 copy-start.7
  0.6 0.0 copy-start.8
  0.7 0.0 copy-start.9
  0.7 0.0 copy-start.4
  0.7 0.0 copy-start.5
  0.7 0.0 copy-start.2
  0.7 0.0 copy-start.3
  0.7 0.0 copy-start
  0.7 0.0 copy-start.1
  0.7 0.0 copy-start.6
  0.7 0.6 copy-done.7
  1.3 0.0 copy-done.8
  1.3 0.0 copy-done.9
  1.3 0.0 copy-done.4
  1.4 0.0 copy-done.5
  1.4 0.0 copy-done.2
  1.4 0.0 copy-done.3
  1.4 0.0 copy-done
  1.4 0.0 copy-done.1
  1.4 0.0 copy-done.6
  1.4 0.4 shard_map.121
  1.9 69.5 %all_to_all.15 = f32[32,1,384]{2,1,0:T(1,128)S(1)} all-to-all(f32[32,1,384]{2,1,0:T(1,128)S(1)} %bitcast.15), channel_id=1, replica_groups=mesh['groups'=2,'pix'=32,'sub'=4,'rep'=2] {'pix'}, dimensions={0} | all-to-all | bytes 98304 | tf_op jit(solution)/shard_map/all_to_all | solution.py:383
  71.3 1.7 %shard_map.122 = (f32[8,16,768]{2,1,0:T(8,128)S(1)}, f32[16,256]{1,0:T(8,128)S(1)}, f32[128,128]{1,0:T(8,128)S(1)}) custom-call(f32[96,128]{1,0:T(8,128)S(1)} %bitcast.14), custom_call_target="tpu_custom_call" | custom-call | tf_op jit(solution)/shard_map/pallas_call | solution.py:384
  73.0 13.6 %all_to_all.16.near = f32[8,16,768]{2,1,0:T(8,128)S(1)} all-to-all(f32[8,16,768]{2,1,0:T(8,128)S(1)} %get-tuple-element.9), channel_id=1, replica_groups=mesh['groups'=2,'pix'=32,'sub'=4,'rep'=2] {'sub','rep'}, dimensions={0} | all-to-all | bytes 786432 | tf_op jit(solution)/shard_map/all_to_all | solution.py:385
  86.6 6.6 %shard_map.123 = f32[32,128]{1,0:T(8,128)S(1)} custom-call(f32[8,16,768]{2,1,0:T(8,128)S(1)} %all_to_all.16.near, f32[16,256]{1,0:T(8,128)S(1)} %get-tuple-element.10.own, f32[128,128]{1,0:T(8,128)S(1)} %get-tuple-element.11.ranks), custom_call_target="tpu_custom_call" | custom-call | tf_op jit(solution)/shard_map/pallas_call | solution.py:386
  93.2 25.3 %all_to_all.17 = f32[32,1,128]{2,1,0:T(1,128)S(1)} all-to-all(f32[32,1,128]{2,1,0:T(1,128)S(1)} %bitcast.16), channel_id=1, replica_groups=mesh['groups'=2,'pix'=32,'sub'=4,'rep'=2] {'pix'}, dimensions={0} | all-to-all | bytes 32768 | tf_op jit(solution)/shard_map/all_to_all | solution.py:387
  118.5 0.8 shard_map.124
Async XLA Ops:
  0.6 0.7 copy-start.7
  0.6 0.7 copy-start.8
  0.7 0.7 copy-start.9
  0.7 0.7 copy-start.4
  0.7 0.7 copy-start.5
  0.7 0.7 copy-start.2
  0.7 0.7 copy-start.3
  0.7 0.7 copy-start
  0.7 0.7 copy-start.1
  0.7 0.7 copy-start.6

commit v2 on v1

--- a/solution.py
+++ b/solution.py
@@ -50,9 +50,17 @@
         body,
         out_shape=outs,
         scratch_shapes=list(scratch),
-        compiler_params=pltpu.CompilerParams(vmem_limit_bytes=8 << 20),
+        compiler_params=pltpu.CompilerParams(vmem_limit_bytes=16 << 20),
         interpret=INTERPRET,
     )
+
+
+def first_peer(pix_count, peers):
+    return peers - pix_count // 2
+
+
+def message_rows(width):
+    return width // LANES * 2 * USED + FIELDS
 
 
 def owners_and_ranks(dest_g, dest_w, sub_count):
@@ -70,8 +78,9 @@
     return own_g, own_w, rank(own_g, columns[:, 0:1]), rank(own_w, columns[:, 1:2])
 
 
-def send_body(pix_count, sub_count):
+def send_body(pix_count, sub_count, peers):
     slots = CAP * sub_count
+    turn = first_peer(pix_count, peers)
 
     def body(gp, gs, gc, gd, gl, wp, ws, wc, wd, wl, msg):
         n = gp.shape[1]
@@ -100,34 +109,39 @@
             left += [jnp.where(rank_g == s, data_g, 0.0), zero]
             right += [zero, jnp.where(rank_w == s, data_w, 0.0)]
         table = jnp.concatenate([jnp.concatenate(left, axis=0), jnp.concatenate(right, axis=0)], axis=1)
-        rows = 3 * pix_count
+        rows = 3 * peers
         r = iota((rows, 2 * n), 0)
-        target = jnp.floor((r.astype(f32) + 0.5) * (1.0 / 3.0)).astype(i32)
-        side = r - 3 * target
+        peer = jnp.floor((r.astype(f32) + 0.5) * (1.0 / 3.0)).astype(i32)
+        side = r - 3 * peer
+        band = (peer - turn) & (peers - 1)
         owner = jnp.concatenate([own_g, own_w], axis=1)
         upper = jnp.concatenate([gl[...], wl[...]], axis=1) >> (NCOL.bit_length() - 1)
-        wanted = (owner == target + side - 1) & ((side == 1) | (upper == jnp.where(side == 0, 1, 0)))
-        pick = one_hot(wanted)
+        edge = (side == 1) | (upper == jnp.where(side == 0, 1, 0))
+        pick = one_hot((owner == band + side - 1) & (band < pix_count) & edge)
         msg[...] = sum(dot(pick, part, ((1,), (1,))) for part in split3(table))
 
     return body
 
 
-def compact_body(pix_count, slots, members, width):
-    own_lanes = pix_count
+def compact_body(peers, slots, members, width):
+    lanes = -(-3 * peers // LANES) * LANES
+    tiles = width // LANES
 
     def body(got, out, own, ranks, chunk):
-        lanes = 3 * pix_count
-        parts = [got[pl.ds(j, pix_count, stride=3), :] for j in (1, 0, 2)]
-        parts.append(jnp.zeros((LANES - lanes, LANES), f32))
+        parts = [got[pl.ds(j, peers, stride=3), :] for j in (1, 0, 2)]
+        parts.append(jnp.zeros((lanes - 3 * peers, LANES), f32))
         data = jnp.transpose(jnp.concatenate(parts, axis=0))
-        lane8 = iota((FIELDS, LANES), 1)
-        row8 = iota((FIELDS, LANES), 0)
-        is_own = lane8 < own_lanes
-        is_low = (lane8 >= own_lanes) & (lane8 < 2 * own_lanes)
-        before = one_hot(iota((LANES, LANES), 0) < iota((LANES, LANES), 1))
+        lane8 = iota((FIELDS, lanes), 1)
+        row8 = iota((FIELDS, lanes), 0)
+        row_of = iota((FIELDS, LANES), 0)
+        is_own = lane8 < peers
+        is_low = (lane8 >= peers) & (lane8 < 2 * peers)
+        before = one_hot(iota((lanes, lanes), 0) < iota((lanes, lanes), 1))
         below = one_hot(iota((slots, slots), 1) < iota((slots, slots), 0))
+        goal = iota((LANES, lanes), 0).astype(f32).astype(bf16)
+        yes, no = jnp.ones((LANES, lanes), bf16), jnp.zeros((LANES, lanes), bf16)
         chunk[...] = jnp.zeros(chunk.shape, f32)
+        own[...] = jnp.zeros(own.shape, f32)
         rank_rows = []
         for c in range(2):
             pieces, codes = [], []
@@ -144,68 +158,85 @@
                 pieces.append(jnp.where(filled, x, 0.0))
                 codes.append(code)
             filled = jnp.concatenate(codes, axis=0) > 0.5
-            flag_own = jnp.where(filled & (iota((slots, LANES), 1) < own_lanes), 1.0, 0.0)
-            flag_far = jnp.where(filled & (iota((slots, LANES), 1) >= own_lanes), 1.0, 0.0)
+            lane_s = iota((slots, lanes), 1)
+            flag_own = jnp.where(filled & (lane_s < peers), 1.0, 0.0)
+            flag_far = jnp.where(filled & (lane_s >= peers), 1.0, 0.0)
 
             def places(flag):
                 inside = dot(flag.astype(bf16), before, ((1,), (0,)))
                 totals = jnp.broadcast_to(jnp.sum(flag, axis=1, keepdims=True), (slots, LANES))
                 ahead = dot(below, totals.astype(bf16), ((1,), (0,)))
-                return inside + ahead, jnp.sum(totals, axis=0, keepdims=True)
+                return inside + ahead[:, 0:1], jnp.sum(totals, axis=0, keepdims=True)
 
             place_own, count_own = places(flag_own)
             place_far, count_far = places(flag_far)
-            place = jnp.where(flag_own > 0.5, place_own, place_far + count_own)
+            place = jnp.where(flag_own > 0.5, place_own, place_far + count_own[:, 0:1])
             place = jnp.where(filled, place, -1.0)
             count = count_own + count_far
-            rank_rows.append(place)
+            rank_rows.append(place[:, 0:LANES])
             stacked = [jnp.concatenate(split3(p), axis=0) for p in pieces]
             total = jnp.max(count)
-            for t in range(width // LANES):
+            for t in range(tiles):
 
                 @pl.when(total > t * LANES)
-                def _(t=t, c=c, place=place, stacked=stacked, count=count, count_own=count_own):
-                    goal = iota((LANES, LANES), 0).astype(f32) + float(t * LANES)
+                def _(t=t, c=c, place=place, stacked=stacked, count_own=count_own):
+                    near_place = (place - float(t * LANES)).astype(bf16)
                     acc = jnp.zeros((3 * FIELDS, LANES), f32)
                     for s in range(slots):
-                        pick = one_hot(goal == place[s : s + 1, :])
+                        pick = jnp.where(goal == near_place[s : s + 1, :], yes, no)
                         acc = acc + dot(stacked[s], pick, ((1,), (1,)))
                     x = acc[0:8, :] + acc[8:16, :] + acc[16:24, :]
-                    x = jnp.where(row8 == 6, count, jnp.where(row8 == 7, count_own, x))
-                    chunk[c * FIELDS : (c + 1) * FIELDS, t * LANES : (t + 1) * LANES] = x
+                    at = t * 2 * USED + c * USED
+                    chunk[at : at + USED, :] = x[0:USED, :]
+                    if t * LANES < own.shape[1]:
+                        x = jnp.where(row_of == 7, count_own, x)
+                        own[c * FIELDS : (c + 1) * FIELDS, t * LANES : (t + 1) * LANES] = x
 
         ranks[...] = jnp.transpose(jnp.concatenate(rank_rows + [jnp.zeros((LANES - 2 * slots, LANES), f32)], axis=0))
         value = chunk[...]
-        own[...] = value[:, : own.shape[1]]
         for d in range(members):
             out[d] = value
 
     return body
 
 
-def match_body(pix_count, slots, members, width):
-    block = 8 * GROUPS
+def prepare_body(peers, slots):
     used = 2 * USED
-    early = 5 * block
-
-    def body(near, own, ranks, out, wide, line, totals):
-        own_width = pix_count * slots
-        lane8 = iota((8, LANES), 1)
+
+    def body(own, ranks, wide, pick):
+        own_width = peers * slots
         stacked = jnp.concatenate([p.astype(f32) for p in split3(own[...])], axis=0)
         columns = jnp.transpose(stacked).astype(bf16)
         spread_to = iota((6 * FIELDS, used * LANES), 1) >> 7
         field_of = spread_to + jnp.where(spread_to >= USED, FIELDS - USED, 0)
         spread = one_hot((iota((6 * FIELDS, used * LANES), 0) & (2 * FIELDS - 1)) == field_of)
-        wide[0:early, :] = dot(columns[0:early, :], spread, ((1,), (0,)))
+        wide[...] = dot(columns, spread, ((1,), (0,)))
+        goal = iota((peers, own_width), 1).astype(f32)
+        for c in range(2):
+            for s in range(slots):
+                rank = ranks[0:peers, c * slots + s : c * slots + s + 1]
+                pick[s * peers : (s + 1) * peers, c * own_width : (c + 1) * own_width] = one_hot(rank == goal)
+
+    return body
+
+
+def match_body(peers, slots, members, width):
+    block = 8 * GROUPS
+    tiles = width // LANES
+    rows = message_rows(width)
+    usual = tiles * 5 // 12
+    own_width = peers * slots
+    early = own_width * 5 // 8
+
+    def body(near, own, wide, pick, out, line, totals, values):
+        lane8 = iota((8, LANES), 1)
         count_own = [jnp.max(own[c * FIELDS + 7 : c * FIELDS + 8, 0:LANES]).astype(i32) for c in range(2)]
 
-        @pl.when(jnp.maximum(count_own[0], count_own[1]) > early)
-        def _():
-            wide[early:own_width, :] = dot(columns[early:own_width, :], spread, ((1,), (0,)))
-
-        counts = [
-            [jnp.max(near[d, c * FIELDS + 6 : c * FIELDS + 7, 0:LANES]).astype(i32) for d in range(members)] for c in range(2)
-        ]
+        def count_of(d, c):
+            codes = near[pl.ds(d * rows + c * USED + USED - 1, tiles, stride=2 * USED), :]
+            return jnp.sum(jnp.where(codes > 0.5, 1.0, 0.0)).astype(i32)
+
+        counts = [[count_of(d, c) for d in range(members)] for c in range(2)]
         ends = []
         for c in range(2):
             start = jnp.int32(0)
@@ -218,25 +249,26 @@
                     line[c, base + k] = x
 
                 def turned(k, c=c, d=d, shift=shift):
-                    return pltpu.roll(near[d, c * FIELDS : (c + 1) * FIELDS, k * LANES : (k + 1) * LANES], shift, 1)
+                    at = d * rows + k * 2 * USED + c * USED
+                    return pltpu.roll(near[at : at + FIELDS, :], shift, 1)
 
                 last = jnp.zeros((FIELDS, LANES), f32) if d == 0 else line[c, base]
-                for k in range(3):
+                for k in range(usual):
                     now = turned(k)
                     put(k, jnp.where(keep, now, last))
                     last = now
-                put(3, jnp.where(keep, 0.0, last))
-                put(4, jnp.zeros((FIELDS, LANES), f32))
-
-                @pl.when(counts[c][d] > 3 * LANES)
+                put(usual, jnp.where(keep, 0.0, last))
+                put(usual + 1, jnp.zeros((FIELDS, LANES), f32))
+
+                @pl.when(counts[c][d] > usual * LANES)
                 def _(c=c, base=base, keep=keep, put=put, turned=turned):
-                    last = line[c, base + 3]
-                    for k in range(3, width // LANES):
+                    last = line[c, base + usual]
+                    for k in range(usual, tiles):
                         now = turned(k)
                         put(k, jnp.where(keep, now, last))
                         last = now
-                    put(width // LANES, jnp.where(keep, 0.0, last))
-                    put(width // LANES + 1, jnp.zeros((FIELDS, LANES), f32))
+                    put(tiles, jnp.where(keep, 0.0, last))
+                    put(tiles + 1, jnp.zeros((FIELDS, LANES), f32))
 
                 start = start + counts[c][d]
             ends.append(lax.div(start + (2 * LANES - 1), 2 * LANES))
@@ -289,39 +321,48 @@
             lax.fori_loop(0, blocks, own_block, 0)
 
         f_of_lane = lane8 & (SLOT_LANES - 1)
-        goal = iota((pix_count, own_width), 1).astype(f32)
-        picks, values = [], []
-        for c in range(2):
-            columns = [ranks[0:pix_count, c * slots + s : c * slots + s + 1] for s in range(slots)]
-            picks.append(jnp.concatenate([one_hot(r == goal) for r in columns], axis=0))
-            rows = []
-            for g in range(own_width // 8):
-                live = (iota((8, LANES), 0) + 8 * g) < count_own[c]
-                value = jnp.zeros((8, LANES), f32)
-                for k in range(3 if c == 0 else 1):
-                    total = jnp.sum(totals[3 * c + k, 8 * g : 8 * g + 8, :], axis=1, keepdims=True) * GAIN
-                    value = jnp.where(f_of_lane == c * FIELDS + k, total, value)
-                rows.append(jnp.where(live, value, 0.0))
-            values.append(jnp.concatenate(rows, axis=0))
-        pick = jnp.concatenate(picks, axis=1)
-        result = sum(dot(pick, part, ((1,), (0,))) for part in split3(jnp.concatenate(values, axis=0)))
-        slot_of_lane = iota((pix_count, LANES), 1) >> 4
-        final = jnp.zeros((pix_count, LANES), f32)
+
+        def sum_rows(first, last):
+            for c in range(2):
+                for g in range(first // 8, last // 8):
+                    live = (iota((8, LANES), 0) + 8 * g) < count_own[c]
+                    value = jnp.zeros((8, LANES), f32)
+                    for k in range(3 if c == 0 else 1):
+                        total = jnp.sum(totals[3 * c + k, 8 * g : 8 * g + 8, :], axis=1, keepdims=True) * GAIN
+                        value = jnp.where(f_of_lane == c * FIELDS + k, total, value)
+                    values[c * own_width + 8 * g : c * own_width + 8 * g + 8, :] = jnp.where(live, value, 0.0)
+
+        many = jnp.maximum(count_own[0], count_own[1]) > early
+        sum_rows(0, early)
+
+        @pl.when(many)
+        def _():
+            sum_rows(early, own_width)
+
+        @pl.when(jnp.logical_not(many))
+        def _():
+            for c in range(2):
+                values[c * own_width + early : (c + 1) * own_width, :] = jnp.zeros((own_width - early, LANES), f32)
+
+        result = sum(dot(pick[...], part, ((1,), (0,))) for part in split3(values[...]))
+        slot_of_lane = iota((peers, LANES), 1) >> 4
+        final = jnp.zeros((peers, LANES), f32)
         for s in range(slots):
-            final = final + jnp.where(slot_of_lane == s, result[s * pix_count : (s + 1) * pix_count, :], 0.0)
+            final = final + jnp.where(slot_of_lane == s, result[s * peers : (s + 1) * peers, :], 0.0)
         out[...] = final
 
     return body
 
 
-def return_body(pix_count, sub_count):
+def return_body(pix_count, sub_count, peers):
     slots = CAP * sub_count
+    turn = first_peer(pix_count, peers)
 
     def body(back, gd, wd, like, offset, wise):
         n = gd.shape[1]
         own_g, own_w, rank_g, rank_w = owners_and_ranks(gd[...], wd[...], sub_count)
         owner = jnp.concatenate([own_g, own_w], axis=1)
-        pick = one_hot(iota((pix_count, 2 * n), 0) == owner)
+        pick = one_hot(iota((peers, 2 * n), 0) == ((owner + turn) & (peers - 1)))
         turned = jnp.transpose(back[...])
         found = sum(dot(part, pick, ((1,), (0,))) for part in split3(turned))
         gaia = jnp.zeros((FIELDS, n), f32)
@@ -337,55 +378,66 @@
     return body
 
 
-def stages(pix_count, sub_count, members, n):
+def stages(pix_count, sub_count, rep_count, n):
+    peers = pix_count * rep_count
     slots = CAP * sub_count
-    width = 3 * pix_count * slots
-    own_width = pix_count * slots
-    send = call(send_body(pix_count, sub_count), jax.ShapeDtypeStruct((3 * pix_count, LANES), f32))
+    width = 3 * peers * slots
+    own_width = peers * slots
+    rows = message_rows(width)
+    send = call(send_body(pix_count, sub_count, peers), jax.ShapeDtypeStruct((3 * peers, LANES), f32))
     compact = call(
-        compact_body(pix_count, slots, members, width),
+        compact_body(peers, slots, sub_count, width),
         (
-            jax.ShapeDtypeStruct((members, 2 * FIELDS, width), f32),
+            jax.ShapeDtypeStruct((sub_count, rows, LANES), f32),
             jax.ShapeDtypeStruct((2 * FIELDS, own_width), f32),
             jax.ShapeDtypeStruct((LANES, LANES), f32),
         ),
-        [pltpu.VMEM((2 * FIELDS, width), f32)],
+        [pltpu.VMEM((rows, LANES), f32)],
+    )
+    prepare = call(
+        prepare_body(peers, slots),
+        (
+            jax.ShapeDtypeStruct((own_width, 2 * USED * LANES), f32),
+            jax.ShapeDtypeStruct((own_width, 2 * own_width), bf16),
+        ),
     )
     match = call(
-        match_body(pix_count, slots, members, width),
-        jax.ShapeDtypeStruct((pix_count, LANES), f32),
+        match_body(peers, slots, sub_count, width),
+        jax.ShapeDtypeStruct((peers, LANES), f32),
         [
-            pltpu.VMEM((own_width, 2 * USED * LANES), f32),
-            pltpu.VMEM((2, members * width // LANES + 8, FIELDS, LANES), f32),
+            pltpu.VMEM((2, sub_count * width // LANES + 8, FIELDS, LANES), f32),
             pltpu.VMEM((4, own_width, LANES), f32),
+            pltpu.VMEM((2 * own_width, LANES), f32),
         ],
     )
     back = call(
-        return_body(pix_count, sub_count),
+        return_body(pix_count, sub_count, peers),
         (
             jax.ShapeDtypeStruct((1, n), f32),
             jax.ShapeDtypeStruct((2, n), f32),
             jax.ShapeDtypeStruct((1, n), f32),
         ),
     )
-    return send, compact, match, back
+    return send, compact, prepare, match, back
 
 
 def shards(gaia_pos, gaia_shape, gaia_corr, gaia_dest, gaia_cell, wise_pos, wise_shape, wise_corr, wise_dest, wise_cell):
     pix_count = lax.axis_size("pix")
     sub_count = lax.axis_size("sub")
-    members = sub_count * lax.axis_size("rep")
+    rep_count = lax.axis_size("rep")
+    peers = pix_count * rep_count
     n = gaia_pos.shape[1]
-    send, compact, match, back = stages(pix_count, sub_count, members, n)
+    send, compact, prepare, match, back = stages(pix_count, sub_count, rep_count, n)
     row = lambda x: x.reshape(1, n)
     gd, wd = row(gaia_dest), row(wise_dest)
     msg = send(gaia_pos, gaia_shape, row(gaia_corr), gd, row(gaia_cell), wise_pos, wise_shape, row(wise_corr), wd, row(wise_cell))
-    got = lax.all_to_all(msg.reshape(pix_count, 1, 3 * LANES), "pix", 0, 0, tiled=True)
-    chunks, own, ranks = compact(got.reshape(3 * pix_count, LANES))
-    near = lax.all_to_all(chunks, ("sub", "rep"), 0, 0, tiled=True)
-    results = match(near, own, ranks)
-    returned = lax.all_to_all(results.reshape(pix_count, 1, LANES), "pix", 0, 0, tiled=True)
-    like, offset, wise = back(returned.reshape(pix_count, LANES), gd, wd)
+    got = lax.all_to_all(msg.reshape(peers, 1, 3 * LANES), ("pix", "rep"), 0, 0, tiled=True)
+    chunks, own, ranks = compact(got.reshape(3 * peers, LANES))
+    near = lax.all_to_all(chunks, "sub", 0, 0, tiled=True)
+    wide, pick = prepare(own, ranks)
+    results = match(near.reshape(-1, LANES), own, wide, pick)
+    returned = lax.all_to_all(results.reshape(peers, 1, LANES), ("pix", "rep"), 0, 0, tiled=True)
+    like, offset, wise = back(returned.reshape(peers, LANES), gd, wd)
     return like.reshape(n), offset, wise.reshape(n)
 
 

time: 120 us -> 140 us (1.17)
  local copies, waits for them, and re-layouts: 0.71 us -> 8.84 us
  waiting for transfers between devices: 0 us -> 5.63 us
  starting transfers between devices: 0 us -> 4.72 us
  Pallas kernels: 9.52 us -> 13 us
    unnamed x20 -> x28, local copies, waits for them, and re-layouts: 0.71 us -> 8.84 us
    all_to_all x0 -> x1, waiting for transfers between devices: none -> 5.63 us  [shards(): near = lax.all_to_all(chunks, 'sub', 0, 0, tiled=True)]
    all_to_all x0 -> x1, starting transfers between devices: none -> 4.72 us  [shards(): near = lax.all_to_all(chunks, 'sub', 0, 0, tiled=True)]
    pallas_call x3 -> x4, Pallas kernels: 9.1 us -> 12.5 us  [the longest x1 7.27 us: shards(): results = match(near.reshape(-1, LANES), own, wide, pick)]
    all_to_all x3 -> x2, blocking collectives: 108 us -> 107 us  [the longest x1 74.8 us: shards(): lax.all_to_all(msg.reshape(peers, 1, 3 * LANES), ('pix', 'rep'), 0, 0, ti...]
  transfers between devices with their start and end apart: 0 -> 1, of which waited for: 0 -> 1; matrix products, arithmetic and copies ran while one was open for 0% -> 0% of each run, Pallas kernels for 0% -> 0%
where the time goes in v2:
time: 140 us
  blocking collectives  107 us (76%)
  Pallas kernels  13 us (9%)
  local copies, waits for them, and re-layouts  8.84 us (6%)
  waiting for transfers between devices  5.63 us (4%)
  starting transfers between devices  4.72 us (3%)
    all_to_all x1, blocking collectives, shards(): lax.all_to_all(msg.reshape(peers, 1, 3 * LANES), ('pix', 'rep'), 0, 0, ti...  74.8 us
    all_to_all x1, blocking collectives, shards(): lax.all_to_all(results.reshape(peers, 1, LANES), ('pix', 'rep'), 0, 0, ti...  32.6 us
    unnamed x28, local copies, waits for them, and re-layouts  8.84 us
    pallas_call x1, Pallas kernels, shards(): results = match(near.reshape(-1, LANES), own, wide, pick)  7.27 us
    all_to_all x1, waiting for transfers between devices, shards(): near = lax.all_to_all(chunks, 'sub', 0, 0, tiled=True)  5.63 us
    all_to_all x1, starting transfers between devices, shards(): near = lax.all_to_all(chunks, 'sub', 0, 0, tiled=True)  4.72 us
    pallas_call x1, Pallas kernels, shards(): chunks, own, ranks = compact(got.reshape(3 * peers, LANES))  3.81 us
  transfers between devices with their start and end apart: 1, of which 1 were waited for; matrix products, arithmetic and copies ran while one was open for 0% of the time, Pallas kernels for 0%

profile of v2, /device:TPU:40, one launch (start us, length us, event | category | flops | bytes accessed | tf_op | source)
XLA Modules:
  0.0 140.3 jit_solution(17223306004029473492)
XLA Ops:
  0.6 0.0 copy-start.2
  0.6 0.6 copy-done.2
  1.3 0.0 copy-start.4
  1.3 0.7 copy-done.4
  1.9 0.0 copy-start.6
  1.9 0.7 copy-done.6
  2.6 0.0 copy-start.7
  2.6 0.7 copy-done.7
  3.3 0.0 copy-start.8
  3.3 0.7 copy-done.8
  4.0 0.0 copy-start.9
  4.0 0.7 copy-done.9
  4.7 0.0 copy-start.10
  4.7 0.7 copy-done.10
  5.3 0.0 copy-start.11
  5.3 0.7 copy-done.11
  6.0 0.0 copy-start.12
  6.0 0.7 copy-done.12
  6.6 0.0 copy-start.13
  6.6 0.7 copy-done.13
  7.3 0.5 shard_map.121
  7.8 74.8 %all_to_all.15 = f32[64,1,384]{2,1,0:T(1,128)S(1)} all-to-all(f32[64,1,384]{2,1,0:T(1,128)S(1)} %bitcast.17), channel_id=1, replica_groups=mesh['groups'=2,'pix'=32,'sub'=4,'rep'=2] {'pix','rep'}, dimensions={0} | all-to-all | bytes 196608 | tf_op jit(solution)/shard_map/all_to_all | solution.py:434
  82.6 3.8 %shard_map.122 = (f32[4,152,128]{2,1,0:T(8,128)}, f32[16,512]{1,0:T(8,128)S(1)}, f32[128,128]{1,0:T(8,128)S(1)}) custom-call(f32[192,128]{1,0:T(8,128)S(1)} %bitcast.16), custom_call_target="tpu_custom_call" | custom-call | tf_op jit(solution)/shard_map/pallas_call | solution.py:435
  86.4 4.7 %all-to-all-start.1 = ((f32[4,152,128]{2,1,0:T(8,128)}), f32[4,152,128]{2,1,0:T(8,128)S(1)}, u32[]{:S(2)}, u32[]{:S(2)}) async-start(f32[4,152,128]{2,1,0:T(8,128)} %get-tuple-element.11), calls=%async_computation.1 | async-start | bytes 622592 | tf_op jit(solution)/shard_map/all_to_all | solution.py:436
  91.1 0.6 shard_map.123
  91.8 0.0 copy-start
  91.8 1.0 copy-done
  92.8 0.0 copy-start.3
  92.8 0.0 copy-start.5
  92.8 5.6 %all-to-all-done.1 = f32[4,152,128]{2,1,0:T(8,128)S(1)} async-done(((f32[4,152,128]{2,1,0:T(8,128)}), f32[4,152,128]{2,1,0:T(8,128)S(1)}, u32[]{:S(2)}, u32[]{:S(2)}) %all-to-all-start.1) | async-done | bytes 311328 | tf_op jit(solution)/shard_map/all_to_all | solution.py:436
  98.4 0.0 copy-start.1
  98.4 1.2 copy-done.1
  99.6 7.3 %shard_map.124 = f32[64,128]{1,0:T(8,128)S(1)} custom-call(f32[608,128]{1,0:T(8,128)S(1)} %bitcast.15, f32[16,512]{1,0:T(8,128)S(1)} %get-tuple-element.12.own, f32[512,1536]{1,0:T(8,128)S(1)} %get-tuple-element.14.wide, bf16[512,1024]{1,0:T(8,128)(2,1)S(1)} %copy-done.1), custom_call_target="tpu_custom_call" | custom-call | tf_op jit(solution)/shard_map/pallas_call | solution.py:438
  106.9 32.6 %all_to_all.16 = f32[64,1,128]{2,1,0:T(1,128)S(1)} all-to-all(f32[64,1,128]{2,1,0:T(1,128)S(1)} %bitcast.18), channel_id=1, replica_groups=mesh['groups'=2,'pix'=32,'sub'=4,'rep'=2] {'pix','rep'}, dimensions={0} | all-to-all | bytes 65536 | tf_op jit(solution)/shard_map/all_to_all | solution.py:439
  139.5 0.0 copy-done.3
  139.5 0.0 copy-done.5
  139.5 0.8 shard_map.125
Async XLA Ops:
  0.6 0.7 copy-start.2
  1.3 0.7 copy-start.4
  1.9 0.7 copy-start.6
  2.6 0.7 copy-start.7
  3.3 0.7 copy-start.8
  4.0 0.7 copy-start.9
  4.7 0.7 copy-start.10
  5.3 0.7 copy-start.11
  6.0 0.7 copy-start.12
  6.6 0.7 copy-start.13
  86.4 12.0 %all-to-all-start.1 = ((f32[4,152,128]{2,1,0:T(8,128)}), f32[4,152,128]{2,1,0:T(8,128)S(1)}, u32[]{:S(2)}, u32[]{:S(2)}) async-start(f32[4,152,128]{2,1,0:T(8,128)} %get-tuple-element.11), calls=%async_computation.1 | async-start | bytes 622592 | tf_op jit(solution)/shard_map/all_to_all | solution.py:436
  91.8 1.0 copy-start
  92.8 46.7 %copy-start.3 = (s32[128,1]{0,1:T(1,128)S(1)}, s32[128,1]{0,1:T(1,128)}, u32[]{:S(2)}) copy-start(s32[128,1]{0,1:T(1,128)} %param.13) | copy-start | bytes 1540
  92.8 46.7 %copy-start.5 = (s32[128,1]{0,1:T(1,128)S(1)}, s32[128,1]{0,1:T(1,128)}, u32[]{:S(2)}) copy-start(s32[128,1]{0,1:T(1,128)} %param.18) | copy-start | bytes 1540
  98.4 1.2 copy-start.1

commit v3 on v2

--- a/solution.py
+++ b/solution.py
@@ -16,7 +16,7 @@
 ROW_BIT = 8192
 LAMBDA = 2.0 * math.log(2.0)
 GAIN = LAMBDA / (2.0 * math.pi)
-GROUPS = 4
+GROUPS = 6
 USED = 6
 INTERPRET = False
 
@@ -45,18 +45,19 @@
     return jnp.where(mask, 1.0, 0.0).astype(bf16)
 
 
-def call(body, outs, scratch=()):
+def call(body, outs, scratch=(), grant=8 << 20, **more):
     return pl.pallas_call(
         body,
         out_shape=outs,
+        **more,
         scratch_shapes=list(scratch),
-        compiler_params=pltpu.CompilerParams(vmem_limit_bytes=16 << 20),
+        compiler_params=pltpu.CompilerParams(vmem_limit_bytes=grant),
         interpret=INTERPRET,
     )
 
 
-def first_peer(pix_count, peers):
-    return peers - pix_count // 2
+def ring_start(pix_count):
+    return pix_count * 3 // 4
 
 
 def message_rows(width):
@@ -80,9 +81,10 @@
 
 def send_body(pix_count, sub_count, peers):
     slots = CAP * sub_count
-    turn = first_peer(pix_count, peers)
-
-    def body(gp, gs, gc, gd, gl, wp, ws, wc, wd, wl, msg):
+    turn = pix_count - ring_start(pix_count)
+
+    def body(*refs):
+        gp, gs, gc, gd, gl, wp, ws, wc, wd, wl, msg, places = refs
         n = gp.shape[1]
         own_g, own_w, rank_g, rank_w = owners_and_ranks(gd[...], wd[...], sub_count)
 
@@ -119,6 +121,8 @@
         edge = (side == 1) | (upper == jnp.where(side == 0, 1, 0))
         pick = one_hot((owner == band + side - 1) & (band < pix_count) & edge)
         msg[...] = sum(dot(pick, part, ((1,), (1,))) for part in split3(table))
+        at = [(o + turn) & (peers - 1) for o in (own_g, own_w)]
+        places[...] = jnp.concatenate(at + [rank_g, rank_w, jnp.zeros((4, n), i32)], axis=0)
 
     return body
 
@@ -210,7 +214,8 @@
         spread_to = iota((6 * FIELDS, used * LANES), 1) >> 7
         field_of = spread_to + jnp.where(spread_to >= USED, FIELDS - USED, 0)
         spread = one_hot((iota((6 * FIELDS, used * LANES), 0) & (2 * FIELDS - 1)) == field_of)
-        wide[...] = dot(columns, spread, ((1,), (0,)))
+        wide[0:own_width, :] = dot(columns, spread, ((1,), (0,)))
+        wide[own_width:, :] = jnp.zeros((8 * GROUPS, used * LANES), f32)
         goal = iota((peers, own_width), 1).astype(f32)
         for c in range(2):
             for s in range(slots):
@@ -224,11 +229,14 @@
     block = 8 * GROUPS
     tiles = width // LANES
     rows = message_rows(width)
-    usual = tiles * 5 // 12
+    usual = tiles // 2
     own_width = peers * slots
     early = own_width * 5 // 8
 
-    def body(near, own, wide, pick, out, line, totals, values):
+    prepare = prepare_body(peers, slots)
+
+    def body(near, own, ranks, out, wide, pick, line, totals, values):
+        prepare(own, ranks, wide, pick)
         lane8 = iota((8, LANES), 1)
         count_own = [jnp.max(own[c * FIELDS + 7 : c * FIELDS + 8, 0:LANES]).astype(i32) for c in range(2)]
 
@@ -354,15 +362,14 @@
     return body
 
 
-def return_body(pix_count, sub_count, peers):
+def return_body(sub_count, peers):
     slots = CAP * sub_count
-    turn = first_peer(pix_count, peers)
-
-    def body(back, gd, wd, like, offset, wise):
-        n = gd.shape[1]
-        own_g, own_w, rank_g, rank_w = owners_and_ranks(gd[...], wd[...], sub_count)
-        owner = jnp.concatenate([own_g, own_w], axis=1)
-        pick = one_hot(iota((peers, 2 * n), 0) == ((owner + turn) & (peers - 1)))
+
+    def body(back, places, like, offset, wise):
+        n = places.shape[1]
+        at = jnp.concatenate([places[0:1, :], places[1:2, :]], axis=1)
+        rank_g, rank_w = places[2:3, :], places[3:4, :]
+        pick = one_hot(iota((peers, 2 * n), 0) == at)
         turned = jnp.transpose(back[...])
         found = sum(dot(part, pick, ((1,), (0,))) for part in split3(turned))
         gaia = jnp.zeros((FIELDS, n), f32)
@@ -379,65 +386,66 @@
 
 
 def stages(pix_count, sub_count, rep_count, n):
-    peers = pix_count * rep_count
+    peers = pix_count
+    members = sub_count * rep_count
     slots = CAP * sub_count
     width = 3 * peers * slots
     own_width = peers * slots
     rows = message_rows(width)
-    send = call(send_body(pix_count, sub_count, peers), jax.ShapeDtypeStruct((3 * peers, LANES), f32))
+    pair, line, whole = pltpu.VMEM((2, n), f32), pltpu.VMEM((1, n), f32), pltpu.VMEM((1, n), i32)
+    send = call(
+        send_body(pix_count, sub_count, peers),
+        (jax.ShapeDtypeStruct((3 * peers, LANES), f32), jax.ShapeDtypeStruct((8, n), i32)),
+    )
     compact = call(
-        compact_body(peers, slots, sub_count, width),
+        compact_body(peers, slots, members, width),
         (
-            jax.ShapeDtypeStruct((sub_count, rows, LANES), f32),
+            jax.ShapeDtypeStruct((members, rows, LANES), f32),
             jax.ShapeDtypeStruct((2 * FIELDS, own_width), f32),
             jax.ShapeDtypeStruct((LANES, LANES), f32),
         ),
         [pltpu.VMEM((rows, LANES), f32)],
     )
-    prepare = call(
-        prepare_body(peers, slots),
-        (
-            jax.ShapeDtypeStruct((own_width, 2 * USED * LANES), f32),
-            jax.ShapeDtypeStruct((own_width, 2 * own_width), bf16),
-        ),
-    )
     match = call(
-        match_body(peers, slots, sub_count, width),
+        match_body(peers, slots, members, width),
         jax.ShapeDtypeStruct((peers, LANES), f32),
         [
-            pltpu.VMEM((2, sub_count * width // LANES + 8, FIELDS, LANES), f32),
-            pltpu.VMEM((4, own_width, LANES), f32),
+            pltpu.VMEM((own_width + 8 * GROUPS, 2 * USED * LANES), f32),
+            pltpu.VMEM((own_width, 2 * own_width), bf16),
+            pltpu.VMEM((2, members * width // LANES + 8, FIELDS, LANES), f32),
+            pltpu.VMEM((4, own_width + 8 * GROUPS, LANES), f32),
             pltpu.VMEM((2 * own_width, LANES), f32),
         ],
     )
     back = call(
-        return_body(pix_count, sub_count, peers),
+        return_body(sub_count, peers),
         (
             jax.ShapeDtypeStruct((1, n), f32),
             jax.ShapeDtypeStruct((2, n), f32),
             jax.ShapeDtypeStruct((1, n), f32),
         ),
     )
-    return send, compact, prepare, match, back
+    return send, compact, match, back
 
 
 def shards(gaia_pos, gaia_shape, gaia_corr, gaia_dest, gaia_cell, wise_pos, wise_shape, wise_corr, wise_dest, wise_cell):
     pix_count = lax.axis_size("pix")
     sub_count = lax.axis_size("sub")
     rep_count = lax.axis_size("rep")
-    peers = pix_count * rep_count
+    peers = pix_count
     n = gaia_pos.shape[1]
-    send, compact, prepare, match, back = stages(pix_count, sub_count, rep_count, n)
+    send, compact, match, back = stages(pix_count, sub_count, rep_count, n)
     row = lambda x: x.reshape(1, n)
     gd, wd = row(gaia_dest), row(wise_dest)
-    msg = send(gaia_pos, gaia_shape, row(gaia_corr), gd, row(gaia_cell), wise_pos, wise_shape, row(wise_corr), wd, row(wise_cell))
-    got = lax.all_to_all(msg.reshape(peers, 1, 3 * LANES), ("pix", "rep"), 0, 0, tiled=True)
+    msg, places = send(gaia_pos, gaia_shape, row(gaia_corr), gd, row(gaia_cell), wise_pos, wise_shape, row(wise_corr), wd, row(wise_cell))
+    ring = [[(i + ring_start(pix_count)) % pix_count for i in range(pix_count)]]
+    exchange = lambda x: lax.all_to_all(x, "pix", 0, 0, axis_index_groups=ring, tiled=True)
+    got = exchange(msg.reshape(peers, 1, 3 * LANES))
     chunks, own, ranks = compact(got.reshape(3 * peers, LANES))
-    near = lax.all_to_all(chunks, "sub", 0, 0, tiled=True)
-    wide, pick = prepare(own, ranks)
-    results = match(near.reshape(-1, LANES), own, wide, pick)
-    returned = lax.all_to_all(results.reshape(peers, 1, LANES), ("pix", "rep"), 0, 0, tiled=True)
-    like, offset, wise = back(returned.reshape(peers, LANES), gd, wd)
+    near = lax.all_to_all(chunks, ("sub", "rep"), 0, 0, tiled=True)
+    results = match(near.reshape(-1, LANES), own, ranks)
+    returned = exchange(results.reshape(peers, 1, LANES))
+    like, offset, wise = back(returned.reshape(peers, LANES), places)
     return like.reshape(n), offset, wise.reshape(n)
 
 

time: 140 us -> 117 us (0.84)
  local copies, waits for them, and re-layouts: 8.84 us -> 0.73 us
  waiting for transfers between devices: 5.63 us -> 0 us
  Pallas kernels: 13 us -> 7.39 us
  starting transfers between devices: 4.72 us -> 0 us
    unnamed x28 -> x20, local copies, waits for them, and re-layouts: 8.84 us -> 0.73 us
    all_to_all x1 -> x0, waiting for transfers between devices: 5.63 us -> none  [shards(): near = lax.all_to_all(chunks, 'sub', 0, 0, tiled=True)]
    all_to_all x1 -> x0, starting transfers between devices: 4.72 us -> none  [shards(): near = lax.all_to_all(chunks, 'sub', 0, 0, tiled=True)]
    pallas_call x3 -> x2, Pallas kernels: 8.72 us -> 5.18 us  [the longest x1 4.36 us: shards(): results = match(near.reshape(-1, LANES), own, ranks)]
    pallas_call x1, Pallas kernels: 3.81 us -> 1.79 us  [shards(): chunks, own, ranks = compact(got.reshape(3 * peers, LANES))]
    all_to_all x2 -> x3, blocking collectives: 107 us -> 107 us  [the longest x2 94.9 us: shards(): lax.all_to_all(x, 'pix', 0, 0, axis_index_groups=ring, tiled=True)]
  transfers between devices with their start and end apart: 1 -> 0, of which waited for: 1 -> 0; matrix products, arithmetic and copies ran while one was open for 0% -> 0% of each run, Pallas kernels for 0% -> 0%
where the time goes in v3:
time: 117 us; the launch traced here: 116 us
  blocking collectives  107 us (91%)
  Pallas kernels  7.39 us (6%)
    all_to_all x2, blocking collectives, shards(): lax.all_to_all(x, 'pix', 0, 0, axis_index_groups=ring, tiled=True)  94.9 us
    all_to_all x1, blocking collectives, shards(): near = lax.all_to_all(chunks, ('sub', 'rep'), 0, 0, tiled=True)  12.6 us
    pallas_call x1, Pallas kernels, shards(): results = match(near.reshape(-1, LANES), own, ranks)  4.36 us

profile of v3, /device:TPU:40, one launch (start us, length us, event | category | flops | bytes accessed | tf_op | source)
XLA Modules:
  0.0 116.3 jit_solution(9597898122884764035)
XLA Ops:
  0.6 0.0 copy-start.7
  0.6 0.0 copy-start.8
  0.7 0.0 copy-start.9
  0.7 0.0 copy-start.3
  0.7 0.0 copy-start.5
  0.7 0.0 copy-start.6
  0.7 0.0 copy-start.1
  0.7 0.0 copy-start.2
  0.7 0.0 copy-start
  0.7 0.0 copy-start.4
  0.7 0.6 copy-done.7
  1.3 0.0 copy-done.8
  1.3 0.0 copy-done.9
  1.3 0.0 copy-done.3
  1.4 0.0 copy-done.5
  1.4 0.0 copy-done.6
  1.4 0.0 copy-done.1
  1.4 0.0 copy-done.2
  1.4 0.0 copy-done
  1.4 0.0 copy-done.4
  1.4 0.4 shard_map.121
  1.9 67.3 %all_to_all.15 = f32[32,1,384]{2,1,0:T(1,128)S(1)} all-to-all(f32[32,1,384]{2,1,0:T(1,128)S(1)} %bitcast.19), channel_id=1, replica_groups={{192,200,208,216,224,232,240,248,0,8,16,24,32,40,48,56,64,72,80,88,96,1..., dimensions={0} | all-to-all | bytes 98304 | tf_op jit(solution)/shard_map/all_to_all | solution.py:442
  69.1 1.8 %shard_map.122 = (f32[8,80,128]{2,1,0:T(8,128)S(1)}, f32[16,256]{1,0:T(8,128)S(1)}, f32[128,128]{1,0:T(8,128)S(1)}) custom-call(f32[96,128]{1,0:T(8,128)S(1)} %bitcast.16), custom_call_target="tpu_custom_call" | custom-call | tf_op jit(solution)/shard_map/pallas_call | solution.py:444
  70.9 12.6 %all_to_all.16 = f32[8,80,128]{2,1,0:T(8,128)S(1)} all-to-all(f32[8,80,128]{2,1,0:T(8,128)S(1)} %get-tuple-element.12), channel_id=1, replica_groups=mesh['groups'=2,'pix'=32,'sub'=4,'rep'=2] {'sub','rep'}, dimensions={0} | all-to-all | bytes 655360 | tf_op jit(solution)/shard_map/all_to_all | solution.py:445
  83.5 4.4 %shard_map.123 = f32[32,128]{1,0:T(8,128)S(1)} custom-call(f32[640,128]{1,0:T(8,128)S(1)} %bitcast.15, f32[16,256]{1,0:T(8,128)S(1)} %get-tuple-element.13.own, f32[128,128]{1,0:T(8,128)S(1)} %get-tuple-element.14.ranks), custom_call_target="tpu_custom_call" | custom-call | tf_op jit(solution)/shard_map/pallas_call | solution.py:446
  87.9 27.6 %all_to_all.17 = f32[32,1,128]{2,1,0:T(1,128)S(1)} all-to-all(f32[32,1,128]{2,1,0:T(1,128)S(1)} %bitcast.18), channel_id=1, replica_groups={{192,200,208,216,224,232,240,248,0,8,16,24,32,40,48,56,64,72,80,88,96,1..., dimensions={0} | all-to-all | bytes 32768 | tf_op jit(solution)/shard_map/all_to_all | solution.py:442
  115.5 0.8 shard_map.124
Async XLA Ops:
  0.6 0.7 copy-start.7
  0.6 0.7 copy-start.8
  0.7 0.7 copy-start.9
  0.7 0.7 copy-start.3
  0.7 0.7 copy-start.5
  0.7 0.7 copy-start.6
  0.7 0.7 copy-start.1
  0.7 0.7 copy-start.2
  0.7 0.7 copy-start
  0.7 0.7 copy-start.4
